TPU v7x, 32 devices: a whole 2x2x4 slice. The times are simulated.
32 devices in a mesh: dp: 2 (over x), sw: 4 (over z), sh: 4 (over y, core).
Axes of the slice: x: 2, y: 2, z: 4, core: 2. Of those that a mesh axis runs over, the one named last changes fastest.
Arguments:
- feat_map: bfloat16 [24, 384, 64, 80], P('dp', 'sh', 'sw'), parts along dimension 0
- norm0_w: bfloat16 [80], replicated
- norm0_b: bfloat16 [80], replicated
- down_w: bfloat16 [2, 2, 80, 160], replicated
- down_b: bfloat16 [160], replicated
- dw_w: bfloat16 [2, 7, 7, 160], replicated
- dw_b: bfloat16 [2, 160], replicated
- norm_w: bfloat16 [2, 160], replicated
- norm_b: bfloat16 [2, 160], replicated
- pw1_w: bfloat16 [2, 160, 640], replicated
- pw1_b: bfloat16 [2, 640], replicated
- pw2_w: bfloat16 [2, 640, 160], replicated
- pw2_b: bfloat16 [2, 160], replicated
- layer_scale: bfloat16 [2, 160], replicated
Outputs:
- output: bfloat16 [24, 192, 32, 160], P('dp', 'sh', 'sw'), parts along dimension 0
There are 2 independent parts. A program takes and returns all parts, laid end to end along the dimension named above; an argument that names none is the same for every part.
All inputs are finite; a program needn't handle non-finite values.
Results may differ from a plain program's by a relative error of at most 0.0119833.
Values are sent between devices in bfloat16 or wider.
A program may use at most 1 GiB of HBM per device.

v0:
```python
import functools

import jax
import jax.numpy as jnp
from jax import lax
from jax.experimental import pallas as pl
from jax.experimental.pallas import tpu as pltpu
from jax.sharding import PartitionSpec as P

LN_EPS = 1e-6
MESH = pl.DeviceIdType.MESH
GI = 4
NPL = GI + 1
LANES = 128
TAIL = 32
ROW = 24
COL0 = 8
BORDER = 3
HALF = 0.5
RSQRT2X2 = 1.4142135623730951

F32 = jnp.float32
BF16 = jnp.bfloat16


def kernel(
    rows_count, cols_count,
    feat, norm0_w, norm0_b, down_w, down_b, dw_w, dw_b, norm_w, norm_b, pw1_w, pw1_b, pw2_w, pw2_b, layer_scale,
    out,
    fv, s0, s1, pad, hsend, hrecv, csend, crecv, cstage, ubuf, vbuf, ybuf, wd, w1, w2, dwf, vec, obuf,
    feat_sem, out_sem, send_sem, recv_sem,
):
    images, _, _, ch_in = fv.shape
    groups = images // GI
    tile_h, tile_w = obuf.shape[1], obuf.shape[2]
    pix = tile_h * tile_w
    my_row, my_col = lax.axis_index("sh"), lax.axis_index("sw")
    has_up, has_down = my_row > 0, my_row < rows_count - 1
    has_left, has_right = my_col > 0, my_col < cols_count - 1

    steps = [(-1, 0), (1, 0), (0, -1), (0, 1), (-1, -1), (-1, 1), (1, -1), (1, 1)]
    row_ok = {-1: has_up, 0: None, 1: has_down}
    col_ok = {-1: has_left, 0: None, 1: has_right}

    def exists(q):
        dr, dc = steps[q]
        if row_ok[dr] is None:
            return col_ok[dc]
        if col_ok[dc] is None:
            return row_ok[dr]
        return jnp.logical_and(row_ok[dr], col_ok[dc])

    def opposite(q):
        dr, dc = steps[q]
        return steps.index((-dr, -dc))

    def device(q):
        dr, dc = steps[q]
        return {"sh": my_row + dr, "sw": my_col + dc}

    feat_copies = [pltpu.make_async_copy(feat.at[i], fv.at[i], feat_sem.at[i]) for i in range(images)]
    for copy in feat_copies:
        copy.start()

    barrier = pltpu.get_barrier_semaphore()
    for q in range(8):
        @pl.when(exists(q))
        def _():
            pl.semaphore_signal(barrier, inc=1, device_id=device(q), device_id_type=MESH)

    def zero_rows(first):
        def body(p, _):
            pad[p, pl.ds(first, BORDER)] = jnp.zeros((BORDER, ROW, LANES), F32)
            return 0
        lax.fori_loop(0, pad.shape[0], body, 0)

    def zero_cols(first):
        def body(p, _):
            pad[p, :, pl.ds(first, 8)] = jnp.zeros((pad.shape[1], 8, LANES), F32)
            return 0
        lax.fori_loop(0, pad.shape[0], body, 0)

    pl.when(jnp.logical_not(has_up))(lambda: zero_rows(0))
    pl.when(jnp.logical_not(has_down))(lambda: zero_rows(BORDER + tile_h))
    pl.when(jnp.logical_not(has_left))(lambda: zero_cols(0))
    pl.when(jnp.logical_not(has_right))(lambda: zero_cols(COL0 + tile_w))

    s0[...] = jnp.zeros(s0.shape, F32)
    s1[...] = jnp.zeros(s1.shape, F32)

    def tail_at(tail, slot):
        rows = tail.shape[0]
        parts = [tail]
        if slot:
            parts = [jnp.zeros((rows, TAIL * slot), tail.dtype)] + parts
        if slot < GI - 1:
            parts = parts + [jnp.zeros((rows, TAIL * (GI - 1 - slot)), tail.dtype)]
        return jnp.concatenate(parts, axis=1)

    for tap in range(4):
        taps = down_w[tap // 2, tap % 2].astype(F32)
        zeros = jnp.zeros((LANES - ch_in, 2 * LANES), BF16)
        for slot in range(GI):
            wd[slot, pl.ds(tap * LANES, ch_in), :LANES] = taps[:, :LANES].astype(BF16)
            wd[slot, pl.ds(tap * LANES, ch_in), LANES:] = tail_at(taps[:, LANES:], slot).astype(BF16)
            wd[slot, pl.ds(tap * LANES + ch_in, LANES - ch_in)] = zeros
    for k in range(2):
        for slot in range(GI):
            w1[k, slot, :LANES] = (pw1_w[k, :LANES, :].astype(F32) * HALF).astype(BF16)
            w1[k, slot, LANES:] = jnp.zeros((LANES, w1.shape[3]), BF16)
            w1[k, slot, pl.ds(LANES + TAIL * slot, TAIL)] = (pw1_w[k, LANES:, :].astype(F32) * HALF).astype(BF16)
            w2[k, slot, :, :LANES] = pw2_w[k, :, :LANES]
            w2[k, slot, :, LANES:] = tail_at(pw2_w[k, :, LANES:].astype(F32), slot).astype(BF16)
        for kh in range(7):
            taps = dw_w[k, kh].astype(F32)
            dwf[k, 0, kh, :7] = taps[:, :LANES]
            dwf[k, 1, kh, :7] = jnp.concatenate([taps[:, LANES:]] * GI, axis=1)

    def split(row):
        row = row.astype(F32)
        return row[:, :LANES], jnp.concatenate([row[:, LANES:]] * GI, axis=1)

    names = [dw_b, norm_w, norm_b, pw2_b, layer_scale]
    for k in range(2):
        for j, ref in enumerate(names):
            head, tail = split(ref[k:k + 1, :])
            vec[k, 0, j:j + 1] = head
            vec[k, 1, j:j + 1] = tail
    head, tail = split(down_b[...])
    vec[0, 0, 5:6] = head
    vec[0, 1, 5:6] = tail

    flat = pad.reshape(pad.shape[0], pad.shape[1] * ROW, LANES)

    def column(plane, row, col, count):
        return flat.at[plane, pl.ds((BORDER + row) * ROW + COL0 + col, count, stride=ROW), :]

    def messages(k, g):
        base = k * groups * NPL + g * NPL
        planes = pl.ds(base, NPL)
        copies = []
        for q, (dr, dc) in enumerate(steps):
            there = opposite(q)
            if dc == 0:
                first = BORDER if dr < 0 else tile_h
                land = BORDER + tile_h if dr < 0 else 0
                src = pad.at[planes, pl.ds(first, BORDER), pl.ds(COL0, tile_w), :]
                dst = pad.at[planes, pl.ds(land, BORDER), pl.ds(COL0, tile_w), :]
            elif dr == 0:
                src = hsend.at[k, g, q - 2]
                dst = hrecv.at[k, g, there - 2]
            else:
                src = csend.at[k, g, q - 4]
                dst = crecv.at[k, g, there - 4]
            copies.append(pltpu.make_async_remote_copy(
                src_ref=src, dst_ref=dst, send_sem=send_sem.at[k, g, q], recv_sem=recv_sem.at[k, g, there],
                device_id=device(q), device_id_type=MESH))
        return copies

    def send(k, g):
        base = k * groups * NPL + g * NPL
        copies = messages(k, g)
        for q in (2, 3):
            first = 0 if q == 2 else tile_w - BORDER

            def fill(p, _):
                for j in range(BORDER):
                    hsend[k, g, q - 2, p * BORDER + j] = column(base + p, 0, first + j, tile_h)[...].astype(BF16)
                return 0

            lax.fori_loop(0, NPL, fill, 0)
        for q in range(4, 8):
            dr, dc = steps[q]
            first = 0 if dc < 0 else tile_w - BORDER
            row = 0 if dr < 0 else tile_h - BORDER
            for p in range(NPL):
                for j in range(BORDER):
                    cstage[pl.ds((p * BORDER + j) * BORDER, BORDER)] = column(base + p, row, first + j, BORDER)[...]
            csend[k, g, q - 4] = cstage[...].astype(BF16)
        for q in range(8):
            pl.when(exists(q))(copies[q].start)

    def receive(k, g):
        base = k * groups * NPL + g * NPL
        copies = messages(k, g)
        for q in range(8):
            pl.when(exists(q))(_wait_recv(k, g, q))
        for q in (2, 3):
            first = -BORDER if q == 2 else tile_w

            @pl.when(exists(q))
            def _():
                def put(p, _):
                    for j in range(BORDER):
                        column(base + p, 0, first + j, tile_h)[...] = hrecv[k, g, q - 2, p * BORDER + j].astype(F32)
                    return 0

                lax.fori_loop(0, NPL, put, 0)
        for q in range(4, 8):
            dr, dc = steps[q]
            first = -BORDER if dc < 0 else tile_w
            row = -BORDER if dr < 0 else tile_h

            @pl.when(exists(q))
            def _():
                cstage[...] = crecv[k, g, q - 4].astype(F32)
                for p in range(NPL):
                    for j in range(BORDER):
                        column(base + p, row, first + j, BORDER)[...] = cstage[pl.ds((p * BORDER + j) * BORDER, BORDER)]

    def _wait_recv(k, g, q):
        base = k * groups * NPL + g * NPL
        dr, dc = steps[q]
        if dc == 0:
            land = 0 if dr < 0 else BORDER + tile_h
            dst = pad.at[pl.ds(base, NPL), pl.ds(land, BORDER), pl.ds(COL0, tile_w), :]
        elif dr == 0:
            dst = hrecv.at[k, g, q - 2]
        else:
            dst = crecv.at[k, g, q - 4]

        def wait():
            pltpu.make_async_remote_copy(
                src_ref=dst, dst_ref=dst, send_sem=send_sem.at[k, g, q], recv_sem=recv_sem.at[k, g, q],
                device_id=device(q), device_id_type=MESH).wait_recv()

        return wait

    def wait_send(k, g):
        copies = messages(k, g)
        for q in range(8):
            pl.when(exists(q))(copies[q].wait_send)

    def interior(plane):
        return pad.at[plane, pl.ds(BORDER, tile_h), pl.ds(COL0, tile_w), :]

    def rounded(values):
        return values.astype(BF16).astype(F32)

    w0 = norm0_w[...].astype(F32)
    b0 = norm0_b[...].astype(F32)

    def down_image(g, i):
        img = g * GI + i
        pltpu.make_async_copy(feat.at[img], fv.at[img], feat_sem.at[img]).wait()
        for kh, stage in ((0, s0), (1, s1)):
            x = fv[img].astype(F32).reshape(tile_h, 2, 2 * tile_w, ch_in)[:, kh].reshape(tile_h * 2 * tile_w, ch_in)
            mean = jnp.sum(x, axis=-1, keepdims=True) * (1.0 / ch_in)
            centered = x - mean
            var = jnp.sum(centered * centered, axis=-1, keepdims=True) * (1.0 / ch_in)
            stage[:, :ch_in] = centered * lax.rsqrt(var + LN_EPS) * w0 + b0
        taps = [s[pl.ds(kw, pix, stride=2), :].astype(BF16) for s in (s0, s1) for kw in (0, 1)]
        d = jnp.dot(jnp.concatenate(taps, axis=1), wd[i], preferred_element_type=F32)
        head = rounded(d[:, :LANES] + vec[0, 0, 5:6])
        interior(g * NPL + i)[...] = head.reshape(tile_h, tile_w, LANES)
        return d[:, LANES:]

    def down_group(g, _):
        ybuf[...] = jnp.zeros(ybuf.shape, F32)

        def one(i, _):
            ybuf[...] += down_image(g, i)
            return 0

        lax.fori_loop(0, GI, one, 0)
        tail = rounded(ybuf[...] + vec[0, 1, 5:6])
        interior(g * NPL + GI)[...] = tail.reshape(tile_h, tile_w, LANES)

        @pl.when(g == 0)
        def _():
            count = jnp.int32(0)
            for q in range(8):
                count = count + exists(q).astype(jnp.int32)
            pl.semaphore_wait(barrier, count)

        send(0, g)
        return 0

    R = 16
    strips = tile_h // R

    def depthwise(k, g):
        base = k * groups * NPL + g * NPL

        def body(t, _):
            p, strip = t // strips, t % strips
            part = (p == GI).astype(jnp.int32)
            r0 = strip * R
            accs = [None] * R
            bias = vec[k, part, 0:1]
            for kw in range(7):
                xs = [pad[base + p, r0 + i, COL0 - BORDER + kw:COL0 - BORDER + kw + 8, :] for i in range(R + 6)]
                for kh in range(7):
                    w = jnp.broadcast_to(dwf[k, part, kh, kw:kw + 1, :], (8, LANES))
                    for r in range(R):
                        term = xs[r + kh] * w
                        accs[r] = term if accs[r] is None else accs[r] + term
            for r in range(R):
                ubuf[p, pl.ds((r0 + r) * 8, 8)] = accs[r] + bias
            return 0

        lax.fori_loop(0, NPL * strips, body, 0)

    LR = 64

    def norm(k):
        nw, nb = vec[k, 0, 1:2], vec[k, 0, 2:3]
        nwt, nbt = vec[k, 1, 1:2], vec[k, 1, 2:3]
        lane = lax.broadcasted_iota(jnp.int32, (LR, LANES), 1)
        channels = LANES + TAIL

        def body(t, _):
            rows = pl.ds(pl.multiple_of(t * LR, LR), LR)
            tail = ubuf[GI, rows]
            heads = [ubuf[i, rows] for i in range(GI)]
            own = [jnp.logical_and(lane >= i * TAIL, lane < (i + 1) * TAIL) for i in range(GI)]

            def pick(cols):
                res = cols[GI - 1]
                for i in range(GI - 2, -1, -1):
                    res = jnp.where(lane < (i + 1) * TAIL, cols[i], res)
                return res

            means = [jnp.sum(heads[i] + jnp.where(own[i], tail, 0.0), axis=-1, keepdims=True) * (1.0 / channels) for i in range(GI)]
            heads = [heads[i] - means[i] for i in range(GI)]
            tail = tail - pick(means)
            square = tail * tail
            rs = [lax.rsqrt(jnp.sum(heads[i] * heads[i] + jnp.where(own[i], square, 0.0), axis=-1, keepdims=True) * (1.0 / channels) + LN_EPS) for i in range(GI)]
            for i in range(GI):
                vbuf[i, rows] = (heads[i] * rs[i] * nw + nb).astype(BF16)
            vbuf[GI, rows] = (tail * pick(rs) * nwt + nbt).astype(BF16)
            return 0

        lax.fori_loop(0, pix // LR, body, 0)

    def mlp(k, g):
        base = k * groups * NPL + g * NPL
        nxt = groups * NPL + g * NPL
        b1 = pw1_b[k:k + 1, :].astype(F32) * HALF
        ybuf[...] = jnp.zeros(ybuf.shape, F32)

        def body(i, _):
            v = jnp.concatenate([vbuf[i], vbuf[GI]], axis=1)
            x = jnp.dot(v, w1[k, i], preferred_element_type=F32) + b1
            hidden = (x + x * lax.erf(x * RSQRT2X2)).astype(BF16)
            y = jnp.dot(hidden, w2[k, i], preferred_element_type=F32)
            head = (y[:, :LANES] + vec[k, 0, 3:4]) * vec[k, 0, 4:5]
            ybuf[...] += y[:, LANES:]
            new = interior(base + i)[...] + head.reshape(tile_h, tile_w, LANES)
            if k == 0:
                interior(nxt + i)[...] = rounded(new)
            else:
                obuf[g * GI + i, :, :, :LANES] = new.astype(BF16)
            return 0

        lax.fori_loop(0, GI, body, 0)
        tail = ((ybuf[...] + vec[k, 1, 3:4]) * vec[k, 1, 4:5]).reshape(tile_h, tile_w, LANES)
        new = interior(base + GI)[...] + tail
        if k == 0:
            interior(nxt + GI)[...] = rounded(new)
        else:
            for i in range(GI):
                obuf[g * GI + i, :, :, LANES:] = new[:, :, i * TAIL:(i + 1) * TAIL].astype(BF16)

    def out_copy(g):
        imgs = pl.ds(g * GI, GI)
        return pltpu.make_async_copy(obuf.at[imgs], out.at[imgs], out_sem.at[g])

    def block_group(k):
        def body(g, _):
            receive(k, g)
            depthwise(k, g)
            norm(k)
            mlp(k, g)
            if k == 0:
                send(1, g)
            else:
                out_copy(g).start()
            return 0
        return body

    lax.fori_loop(0, groups, down_group, 0)
    lax.fori_loop(0, groups, block_group(0), 0)
    lax.fori_loop(0, groups, block_group(1), 0)

    def finish(g, _):
        wait_send(0, g)
        wait_send(1, g)
        out_copy(g).wait()
        return 0

    lax.fori_loop(0, groups, finish, 0)


def solution(mesh):
    rows_count = mesh.shape["sh"]
    cols_count = mesh.shape["sw"]
    act_spec = P("dp", "sh", "sw", None)

    def local_run(feat_map, norm0_w, norm0_b, down_w, down_b, dw_w, dw_b, norm_w, norm_b, pw1_w, pw1_b, pw2_w, pw2_b, layer_scale):
        images, in_h, in_w, ch_in = feat_map.shape
        tile_h, tile_w = in_h // 2, in_w // 2
        ch, hidden = pw1_w.shape[1:]
        groups = images // GI
        pix = tile_h * tile_w
        vmem = pl.BlockSpec(memory_space=pltpu.VMEM)
        hbm = pl.BlockSpec(memory_space=pl.ANY)
        return pl.pallas_call(
            functools.partial(kernel, rows_count, cols_count),
            out_shape=jax.ShapeDtypeStruct((images, tile_h, tile_w, ch), BF16),
            in_specs=[hbm] + [vmem] * 13,
            out_specs=hbm,
            scratch_shapes=[
                pltpu.VMEM((images, in_h, in_w, ch_in), BF16),
                pltpu.VMEM((2 * pix, LANES), F32),
                pltpu.VMEM((2 * pix, LANES), F32),
                pltpu.VMEM((2 * groups * NPL, tile_h + 2 * BORDER, ROW, LANES), F32),
                pltpu.VMEM((2, groups, 2, NPL * BORDER, tile_h, LANES), BF16),
                pltpu.VMEM((2, groups, 2, NPL * BORDER, tile_h, LANES), BF16),
                pltpu.VMEM((2, groups, 4, 48, LANES), BF16),
                pltpu.VMEM((2, groups, 4, 48, LANES), BF16),
                pltpu.VMEM((48, LANES), F32),
                pltpu.VMEM((NPL, pix, LANES), F32),
                pltpu.VMEM((NPL, pix, LANES), BF16),
                pltpu.VMEM((pix, LANES), F32),
                pltpu.VMEM((GI, 4 * LANES, 2 * LANES), BF16),
                pltpu.VMEM((2, GI, 2 * LANES, hidden), BF16),
                pltpu.VMEM((2, GI, hidden, 2 * LANES), BF16),
                pltpu.VMEM((2, 2, 7, 8, LANES), F32),
                pltpu.VMEM((2, 2, 8, LANES), F32),
                pltpu.VMEM((images, tile_h, tile_w, ch), BF16),
                pltpu.SemaphoreType.DMA((images,)),
                pltpu.SemaphoreType.DMA((groups,)),
                pltpu.SemaphoreType.DMA((2, groups, 8)),
                pltpu.SemaphoreType.DMA((2, groups, 8)),
            ],
            compiler_params=pltpu.CompilerParams(collective_id=0, has_side_effects=True, vmem_limit_bytes=63 * 1024 * 1024),
        )(feat_map, norm0_w.reshape(1, -1), norm0_b.reshape(1, -1), down_w, down_b.reshape(1, -1), dw_w, dw_b, norm_w, norm_b, pw1_w, pw1_b, pw2_w, pw2_b, layer_scale)

    return jax.shard_map(local_run, mesh=mesh, in_specs=(act_spec,) + (P(),) * 13, out_specs=act_spec, check_vma=False)
```

profile of v0, /device:TPU:1, one launch (start us, length us, event | category | flops | bytes accessed | tf_op | source)
XLA Modules:
  0.0 83.6 jit_solution(6010525849365838404)
XLA Ops:
  0.0 1.3 %reshape.11.down_b = bf16[1,160]{1,0:T(2,128)(2,1)} reshape(bf16[160]{0:T(256)(128)(2,1)} %param.18) | data formatting | bytes 640 | tf_op jit(solution)/shard_map/reshape | solution.py:438
  1.3 1.4 %copy.16.dw_w = bf16[2,7,7,160]{3,2,1,0:T(8,128)(2,1)} copy(bf16[2,7,7,160]{3,0,2,1:T(2,128)(2,1)} %param.19) | data formatting | bytes 62720 | tf_op args[5]
  2.7 2.1 %copy.17.pw2_w = bf16[2,640,160]{2,1,0:T(8,128)(2,1)} copy(bf16[2,640,160]{1,2,0:T(8,128)(2,1)} %param.25) | data formatting | bytes 819200 | tf_op args[11]
  4.7 7.1 %copy.15.feat = bf16[12,96,16,80]{3,2,1,0:T(8,128)(2,1)} copy(bf16[12,96,16,80]{1,3,2,0:T(8,128)(2,1)} %param.14) | data formatting | bytes 5898240 | tf_op args[0]
  11.8 68.5 %shard_map.136 = bf16[12,48,8,160]{3,2,1,0:T(8,128)(2,1)} custom-call(bf16[12,96,16,80]{3,2,1,0:T(8,128)(2,1)} %copy.15.feat, bf16[1,80]{1,0:T(2,128)(2,1)} %bitcast.2, bf16[1,80]{1,0:T(2,128)(2,1)} %bitcast.3, bf16[2,2,80,160]{3,2,1,0:T(8,128)(2,1)} %down_w.1, bf16[1,160]{1,0:T(2,128)(2,1)} %reshape.11.down_b, bf16[2,7,7,160]{3,2,1,0:T(8,128)(2,1)} %copy.16.dw_w, ...), custom_call_target="tpu_custom_call" | custom-call | tf_op jit(solution)/shard_map/pallas_call | solution.py:408
  80.4 3.2 %copy.19 = bf16[12,48,8,160]{3,2,1,0:T(8,128)(2,1)} copy(bf16[12,48,8,160]{3,2,1,0:T(8,128)(2,1)} %shard_map.136) | data formatting | bytes 2949120
where the time goes:
time: 84.2 us; the launch traced here: 83.6 us
  Pallas kernels  68.5 us (81%)
  local copies, waits for them, and re-layouts  15.1 us (18%)
    pallas_call x1, Pallas kernels, local_run(): pl.pallas_call(functools.partial(kernel, rows_count, cols_count), out_sha...  68.5 us
    unnamed x4, local copies, waits for them, and re-layouts  13.8 us

commit v1 on v0

--- a/solution.py
+++ b/solution.py
@@ -27,10 +27,10 @@
     rows_count, cols_count,
     feat, norm0_w, norm0_b, down_w, down_b, dw_w, dw_b, norm_w, norm_b, pw1_w, pw1_b, pw2_w, pw2_b, layer_scale,
     out,
-    fv, s0, s1, pad, hsend, hrecv, csend, crecv, cstage, ubuf, vbuf, ybuf, wd, w1, w2, dwf, vec, obuf,
+    fv, ab, sel, norm0, pad, hsend, hrecv, csend, crecv, cstage, ubuf, vbuf, ybuf, wd, w1, w2, dwf, vec, obuf,
     feat_sem, out_sem, send_sem, recv_sem,
 ):
-    images, _, _, ch_in = fv.shape
+    images, in_w, ch_in, in_h = fv.shape
     groups = images // GI
     tile_h, tile_w = obuf.shape[1], obuf.shape[2]
     pix = tile_h * tile_w
@@ -85,8 +85,14 @@
     pl.when(jnp.logical_not(has_left))(lambda: zero_cols(0))
     pl.when(jnp.logical_not(has_right))(lambda: zero_cols(COL0 + tile_w))
 
-    s0[...] = jnp.zeros(s0.shape, F32)
-    s1[...] = jnp.zeros(s1.shape, F32)
+    ab[...] = jnp.zeros(ab.shape, BF16)
+    row_id = lax.broadcasted_iota(jnp.int32, sel.shape, 0)
+    col_id = lax.broadcasted_iota(jnp.int32, sel.shape, 1)
+    picked = jnp.where(row_id < tile_h, 2 * row_id, 2 * (row_id - tile_h) + 1)
+    sel[...] = jnp.where(col_id == picked, 1.0, 0.0).astype(BF16)
+    norm0[0] = jnp.broadcast_to(norm0_w[...].astype(F32), (LANES, ch_in)).T
+    norm0[1] = jnp.broadcast_to(norm0_b[...].astype(F32), (LANES, ch_in)).T
+    cstage[...] = jnp.zeros(cstage.shape, F32)
 
     def tail_at(tail, slot):
         rows = tail.shape[0]
@@ -109,12 +115,17 @@
             w1[k, slot, :LANES] = (pw1_w[k, :LANES, :].astype(F32) * HALF).astype(BF16)
             w1[k, slot, LANES:] = jnp.zeros((LANES, w1.shape[3]), BF16)
             w1[k, slot, pl.ds(LANES + TAIL * slot, TAIL)] = (pw1_w[k, LANES:, :].astype(F32) * HALF).astype(BF16)
-            w2[k, slot, :, :LANES] = pw2_w[k, :, :LANES]
-            w2[k, slot, :, LANES:] = tail_at(pw2_w[k, :, LANES:].astype(F32), slot).astype(BF16)
-        for kh in range(7):
-            taps = dw_w[k, kh].astype(F32)
-            dwf[k, 0, kh, :7] = taps[:, :LANES]
-            dwf[k, 1, kh, :7] = jnp.concatenate([taps[:, LANES:]] * GI, axis=1)
+            w2[k, slot, :LANES] = pw2_w[k, :LANES, :]
+            w2[k, slot, LANES:] = jnp.zeros((LANES, w2.shape[3]), BF16)
+            w2[k, slot, pl.ds(LANES + TAIL * slot, TAIL)] = pw2_w[k, LANES:, :]
+
+    for kh in range(7):
+        for kw in range(7):
+            taps = dw_w[kh, kw].astype(F32)
+            tails = jnp.concatenate([taps[:, LANES:]] * GI, axis=1)
+            for k in range(2):
+                dwf[k, 0, kh, kw:kw + 1] = taps[k:k + 1, :LANES]
+                dwf[k, 1, kh, kw:kw + 1] = tails[k:k + 1]
 
     def split(row):
         row = row.astype(F32)
@@ -126,7 +137,7 @@
             head, tail = split(ref[k:k + 1, :])
             vec[k, 0, j:j + 1] = head
             vec[k, 1, j:j + 1] = tail
-    head, tail = split(down_b[...])
+    head, tail = split(down_b[...].reshape(1, -1))
     vec[0, 0, 5:6] = head
     vec[0, 1, 5:6] = tail
 
@@ -182,7 +193,6 @@
 
     def receive(k, g):
         base = k * groups * NPL + g * NPL
-        copies = messages(k, g)
         for q in range(8):
             pl.when(exists(q))(_wait_recv(k, g, q))
         for q in (2, 3):
@@ -237,22 +247,22 @@
     def rounded(values):
         return values.astype(BF16).astype(F32)
 
-    w0 = norm0_w[...].astype(F32)
-    b0 = norm0_b[...].astype(F32)
-
     def down_image(g, i):
         img = g * GI + i
         pltpu.make_async_copy(feat.at[img], fv.at[img], feat_sem.at[img]).wait()
-        for kh, stage in ((0, s0), (1, s1)):
-            x = fv[img].astype(F32).reshape(tile_h, 2, 2 * tile_w, ch_in)[:, kh].reshape(tile_h * 2 * tile_w, ch_in)
-            mean = jnp.sum(x, axis=-1, keepdims=True) * (1.0 / ch_in)
+        for w in range(in_w):
+            x = fv[img, w].astype(F32)
+            mean = jnp.sum(x, axis=0, keepdims=True) * (1.0 / ch_in)
             centered = x - mean
-            var = jnp.sum(centered * centered, axis=-1, keepdims=True) * (1.0 / ch_in)
-            stage[:, :ch_in] = centered * lax.rsqrt(var + LN_EPS) * w0 + b0
-        taps = [s[pl.ds(kw, pix, stride=2), :].astype(BF16) for s in (s0, s1) for kw in (0, 1)]
-        d = jnp.dot(jnp.concatenate(taps, axis=1), wd[i], preferred_element_type=F32)
+            var = jnp.sum(centered * centered, axis=0, keepdims=True) * (1.0 / ch_in)
+            a = centered * lax.rsqrt(var + LN_EPS) * norm0[0, :, :in_h] + norm0[1, :, :in_h]
+            ab[pl.ds(w * LANES, ch_in), :in_h] = a.astype(BF16)
+        turned = lax.dot_general(sel[...], ab[...], (((1,), (1,)), ((), ())), preferred_element_type=F32).astype(BF16)
+        taps = [jnp.concatenate([turned[:tile_h, w * 2 * LANES:(w + 1) * 2 * LANES], turned[tile_h:, w * 2 * LANES:(w + 1) * 2 * LANES]], axis=1) for w in range(tile_w)]
+        d = jnp.dot(jnp.concatenate(taps, axis=0), wd[i], preferred_element_type=F32)
         head = rounded(d[:, :LANES] + vec[0, 0, 5:6])
-        interior(g * NPL + i)[...] = head.reshape(tile_h, tile_w, LANES)
+        for w in range(tile_w):
+            column(g * NPL + i, 0, w, tile_h)[...] = head[w * tile_h:(w + 1) * tile_h]
         return d[:, LANES:]
 
     def down_group(g, _):
@@ -264,7 +274,8 @@
 
         lax.fori_loop(0, GI, one, 0)
         tail = rounded(ybuf[...] + vec[0, 1, 5:6])
-        interior(g * NPL + GI)[...] = tail.reshape(tile_h, tile_w, LANES)
+        for w in range(tile_w):
+            column(g * NPL + GI, 0, w, tile_h)[...] = tail[w * tile_h:(w + 1) * tile_h]
 
         @pl.when(g == 0)
         def _():
@@ -343,7 +354,7 @@
             v = jnp.concatenate([vbuf[i], vbuf[GI]], axis=1)
             x = jnp.dot(v, w1[k, i], preferred_element_type=F32) + b1
             hidden = (x + x * lax.erf(x * RSQRT2X2)).astype(BF16)
-            y = jnp.dot(hidden, w2[k, i], preferred_element_type=F32)
+            y = lax.dot_general(hidden, w2[k, i], (((1,), (1,)), ((), ())), preferred_element_type=F32)
             head = (y[:, :LANES] + vec[k, 0, 3:4]) * vec[k, 0, 4:5]
             ybuf[...] += y[:, LANES:]
             new = interior(base + i)[...] + head.reshape(tile_h, tile_w, LANES)
@@ -411,9 +422,10 @@
             in_specs=[hbm] + [vmem] * 13,
             out_specs=hbm,
             scratch_shapes=[
-                pltpu.VMEM((images, in_h, in_w, ch_in), BF16),
-                pltpu.VMEM((2 * pix, LANES), F32),
-                pltpu.VMEM((2 * pix, LANES), F32),
+                pltpu.VMEM((images, in_w, ch_in, in_h), BF16),
+                pltpu.VMEM((in_w * LANES, LANES), BF16),
+                pltpu.VMEM((in_h, LANES), BF16),
+                pltpu.VMEM((2, ch_in, LANES), F32),
                 pltpu.VMEM((2 * groups * NPL, tile_h + 2 * BORDER, ROW, LANES), F32),
                 pltpu.VMEM((2, groups, 2, NPL * BORDER, tile_h, LANES), BF16),
                 pltpu.VMEM((2, groups, 2, NPL * BORDER, tile_h, LANES), BF16),
@@ -425,7 +437,7 @@
                 pltpu.VMEM((pix, LANES), F32),
                 pltpu.VMEM((GI, 4 * LANES, 2 * LANES), BF16),
                 pltpu.VMEM((2, GI, 2 * LANES, hidden), BF16),
-                pltpu.VMEM((2, GI, hidden, 2 * LANES), BF16),
+                pltpu.VMEM((2, GI, 2 * LANES, hidden), BF16),
                 pltpu.VMEM((2, 2, 7, 8, LANES), F32),
                 pltpu.VMEM((2, 2, 8, LANES), F32),
                 pltpu.VMEM((images, tile_h, tile_w, ch), BF16),
@@ -435,6 +447,9 @@
                 pltpu.SemaphoreType.DMA((2, groups, 8)),
             ],
             compiler_params=pltpu.CompilerParams(collective_id=0, has_side_effects=True, vmem_limit_bytes=63 * 1024 * 1024),
-        )(feat_map, norm0_w.reshape(1, -1), norm0_b.reshape(1, -1), down_w, down_b.reshape(1, -1), dw_w, dw_b, norm_w, norm_b, pw1_w, pw1_b, pw2_w, pw2_b, layer_scale)
+        )(
+            feat_map.transpose(0, 2, 3, 1), norm0_w.reshape(1, -1), norm0_b.reshape(1, -1), down_w, down_b, dw_w.transpose(1, 2, 0, 3), dw_b,
+            norm_w, norm_b, pw1_w, pw1_b, pw2_w.transpose(0, 2, 1), pw2_b, layer_scale,
+        )
 
     return jax.shard_map(local_run, mesh=mesh, in_specs=(act_spec,) + (P(),) * 13, out_specs=act_spec, check_vma=False)

time: 84.2 us -> 69.4 us (0.82)
  local copies, waits for them, and re-layouts: 15.1 us -> 3.22 us
  Pallas kernels: 68.5 us -> 65.8 us
    unnamed x4 -> x1, local copies, waits for them, and re-layouts: 13.8 us -> 3.22 us
    pallas_call x1, Pallas kernels: 68.5 us -> 65.8 us  [local_run(): pl.pallas_call(functools.partial(kernel, rows_count, cols_count), out_sha...]
    reshape x1 -> x0, local copies, waits for them, and re-layouts: 1.25 us -> none  [local_run(): down_b.reshape(1, -1)]
where the time goes in v1:
time: 69.4 us; the launch traced here: 69 us
  Pallas kernels  65.8 us (95%)
  local copies, waits for them, and re-layouts  3.22 us (5%)
    pallas_call x1, Pallas kernels, local_run(): pl.pallas_call(functools.partial(kernel, rows_count, cols_count), out_sha...  65.8 us
    unnamed x1, local copies, waits for them, and re-layouts  3.22 us

profile of v1, /device:TPU:1, one launch (start us, length us, event | category | flops | bytes accessed | tf_op | source)
XLA Modules:
  0.0 69.0 jit_solution(6358653708145918423)
XLA Ops:
  0.0 65.8 %shard_map.136 = bf16[12,48,8,160]{3,2,1,0:T(8,128)(2,1)} custom-call(bf16[12,16,80,96]{3,2,1,0:T(8,128)(2,1)} %bitcast.5, bf16[1,80]{1,0:T(2,128)(2,1)} %bitcast.8, bf16[1,80]{1,0:T(2,128)(2,1)} %bitcast.9, bf16[2,2,80,160]{3,2,1,0:T(8,128)(2,1)} %down_w.1, bf16[160]{0:T(256)(128)(2,1)} %down_b.1, bf16[7,7,2,160]{3,2,1,0:T(2,128)(2,1)} %bitcast.7, ...), custom_call_target="tpu_custom_call" | custom-call | tf_op jit(solution)/shard_map/pallas_call | solution.py:419
  65.8 3.2 %copy.16 = bf16[12,48,8,160]{3,2,1,0:T(8,128)(2,1)} copy(bf16[12,48,8,160]{3,2,1,0:T(8,128)(2,1)} %shard_map.136) | data formatting | bytes 2949120

commit v2 on v1

--- a/solution.py
+++ b/solution.py
@@ -27,8 +27,8 @@
     rows_count, cols_count,
     feat, norm0_w, norm0_b, down_w, down_b, dw_w, dw_b, norm_w, norm_b, pw1_w, pw1_b, pw2_w, pw2_b, layer_scale,
     out,
-    fv, ab, sel, norm0, pad, hsend, hrecv, csend, crecv, cstage, ubuf, vbuf, ybuf, wd, w1, w2, dwf, vec, obuf,
-    feat_sem, out_sem, send_sem, recv_sem,
+    fv, ab, sel, norm0, pad, hsend, hrecv, csend, crecv, cstage, ubuf, vbuf, ybuf, wd, wdt, pw1, pw2, w1, w1t, w2t, dwf, eye, diag, vec, obuf,
+    feat_sem, weight_sem, out_sem, send_sem, recv_sem,
 ):
     images, in_w, ch_in, in_h = fv.shape
     groups = images // GI
@@ -59,7 +59,8 @@
         return {"sh": my_row + dr, "sw": my_col + dc}
 
     feat_copies = [pltpu.make_async_copy(feat.at[i], fv.at[i], feat_sem.at[i]) for i in range(images)]
-    for copy in feat_copies:
+    weight_copies = [pltpu.make_async_copy(pw1_w, pw1, weight_sem.at[0]), pltpu.make_async_copy(pw2_w, pw2, weight_sem.at[1])]
+    for copy in feat_copies[:GI] + weight_copies + feat_copies[GI:]:
         copy.start()
 
     barrier = pltpu.get_barrier_semaphore()
@@ -105,19 +106,25 @@
 
     for tap in range(4):
         taps = down_w[tap // 2, tap % 2].astype(F32)
-        zeros = jnp.zeros((LANES - ch_in, 2 * LANES), BF16)
+        zeros = jnp.zeros((LANES - ch_in, LANES), BF16)
+        wd[pl.ds(tap * LANES, ch_in)] = taps[:, :LANES].astype(BF16)
+        wd[pl.ds(tap * LANES + ch_in, LANES - ch_in)] = zeros
         for slot in range(GI):
-            wd[slot, pl.ds(tap * LANES, ch_in), :LANES] = taps[:, :LANES].astype(BF16)
-            wd[slot, pl.ds(tap * LANES, ch_in), LANES:] = tail_at(taps[:, LANES:], slot).astype(BF16)
-            wd[slot, pl.ds(tap * LANES + ch_in, LANES - ch_in)] = zeros
-    for k in range(2):
-        for slot in range(GI):
-            w1[k, slot, :LANES] = (pw1_w[k, :LANES, :].astype(F32) * HALF).astype(BF16)
-            w1[k, slot, LANES:] = jnp.zeros((LANES, w1.shape[3]), BF16)
-            w1[k, slot, pl.ds(LANES + TAIL * slot, TAIL)] = (pw1_w[k, LANES:, :].astype(F32) * HALF).astype(BF16)
-            w2[k, slot, :LANES] = pw2_w[k, :LANES, :]
-            w2[k, slot, LANES:] = jnp.zeros((LANES, w2.shape[3]), BF16)
-            w2[k, slot, pl.ds(LANES + TAIL * slot, TAIL)] = pw2_w[k, LANES:, :]
+            wdt[slot, pl.ds(tap * LANES, ch_in)] = tail_at(taps[:, LANES:], slot).astype(BF16)
+            wdt[slot, pl.ds(tap * LANES + ch_in, LANES - ch_in)] = zeros
+
+    def block_weights():
+        for copy in weight_copies:
+            copy.wait()
+        for k in range(2):
+            w1[k] = (pw1[k, :LANES].astype(F32) * HALF).astype(BF16)
+            up_tail = (pw1[k, LANES:].astype(F32) * HALF).astype(BF16)
+            for slot in range(GI):
+                for other in range(GI):
+                    rows = pl.ds(TAIL * other, TAIL)
+                    w1t[k, slot, rows] = up_tail if other == slot else jnp.zeros(up_tail.shape, BF16)
+                    w2t[k, slot, rows] = pw2[k, LANES:] if other == slot else jnp.zeros(up_tail.shape, BF16)
+        lax.fori_loop(0, 7, spread, 0)
 
     for kh in range(7):
         for kw in range(7):
@@ -126,6 +133,22 @@
             for k in range(2):
                 dwf[k, 0, kh, kw:kw + 1] = taps[k:k + 1, :LANES]
                 dwf[k, 1, kh, kw:kw + 1] = tails[k:k + 1]
+
+    eye[...] = jnp.where(lax.broadcasted_iota(jnp.int32, eye.shape, 0) == lax.broadcasted_iota(jnp.int32, eye.shape, 1), 1.0, 0.0).astype(BF16)
+
+    def spread(kw, _):
+        unit = eye[...]
+        for k in range(2):
+            for kh in range(8):
+                if kh < 7:
+                    tap = jnp.broadcast_to(dwf[k, 0, kh, pl.ds(kw, 1)], (16, LANES)).astype(BF16)
+                    block = unit * jnp.concatenate([tap] * (LANES // 16), axis=0)
+                else:
+                    block = jnp.zeros((LANES, LANES), BF16)
+                diag[k, pl.ds(pl.multiple_of(kw * 4 * LANES, LANES) + kh // 2 * LANES, LANES), kh % 2 * LANES:(kh % 2 + 1) * LANES] = block
+        return 0
+
+    pad[:, tile_h + 2 * BORDER:] = jnp.zeros((pad.shape[0], 2, ROW, LANES), F32)
 
     def split(row):
         row = row.astype(F32)
@@ -247,7 +270,7 @@
     def rounded(values):
         return values.astype(BF16).astype(F32)
 
-    def down_image(g, i):
+    def down_norm(g, i, slot):
         img = g * GI + i
         pltpu.make_async_copy(feat.at[img], fv.at[img], feat_sem.at[img]).wait()
         for w in range(in_w):
@@ -256,23 +279,29 @@
             centered = x - mean
             var = jnp.sum(centered * centered, axis=0, keepdims=True) * (1.0 / ch_in)
             a = centered * lax.rsqrt(var + LN_EPS) * norm0[0, :, :in_h] + norm0[1, :, :in_h]
-            ab[pl.ds(w * LANES, ch_in), :in_h] = a.astype(BF16)
-        turned = lax.dot_general(sel[...], ab[...], (((1,), (1,)), ((), ())), preferred_element_type=F32).astype(BF16)
+            ab[slot, pl.ds(w * LANES, ch_in), :in_h] = a.astype(BF16)
+
+    def down_conv(g, i, slot):
+        turned = lax.dot_general(sel[...], ab[slot], (((1,), (1,)), ((), ())), preferred_element_type=F32).astype(BF16)
         taps = [jnp.concatenate([turned[:tile_h, w * 2 * LANES:(w + 1) * 2 * LANES], turned[tile_h:, w * 2 * LANES:(w + 1) * 2 * LANES]], axis=1) for w in range(tile_w)]
-        d = jnp.dot(jnp.concatenate(taps, axis=0), wd[i], preferred_element_type=F32)
+        weights = jnp.concatenate([wd[...], wdt[i]], axis=1)
+        d = jnp.dot(jnp.concatenate(taps, axis=0), weights, preferred_element_type=F32)
         head = rounded(d[:, :LANES] + vec[0, 0, 5:6])
         for w in range(tile_w):
             column(g * NPL + i, 0, w, tile_h)[...] = head[w * tile_h:(w + 1) * tile_h]
-        return d[:, LANES:]
+        ybuf[...] += d[:, LANES:]
 
     def down_group(g, _):
         ybuf[...] = jnp.zeros(ybuf.shape, F32)
 
-        def one(i, _):
-            ybuf[...] += down_image(g, i)
-            return 0
-
-        lax.fori_loop(0, GI, one, 0)
+        def two(j, _):
+            down_norm(g, 2 * j, 0)
+            down_norm(g, 2 * j + 1, 1)
+            down_conv(g, 2 * j, 0)
+            down_conv(g, 2 * j + 1, 1)
+            return 0
+
+        lax.fori_loop(0, GI // 2, two, 0)
         tail = rounded(ybuf[...] + vec[0, 1, 5:6])
         for w in range(tile_w):
             column(g * NPL + GI, 0, w, tile_h)[...] = tail[w * tile_h:(w + 1) * tile_h]
@@ -287,30 +316,43 @@
         send(0, g)
         return 0
 
-    R = 16
-    strips = tile_h // R
+    half = tile_h // 2
+
+    def taps_sum(k, part, plane, r0, count):
+        accs = [None] * count
+        for kw in range(7):
+            xs = [pad[plane, r0 + i, COL0 - BORDER + kw:COL0 - BORDER + kw + 8, :] for i in range(count + 6)]
+            for kh in range(7):
+                w = jnp.broadcast_to(dwf[k, part, kh, kw:kw + 1, :], (8, LANES))
+                for r in range(count):
+                    term = xs[r + kh] * w
+                    accs[r] = term if accs[r] is None else accs[r] + term
+        return accs
 
     def depthwise(k, g):
         base = k * groups * NPL + g * NPL
-
-        def body(t, _):
-            p, strip = t // strips, t % strips
-            part = (p == GI).astype(jnp.int32)
-            r0 = strip * R
-            accs = [None] * R
-            bias = vec[k, part, 0:1]
-            for kw in range(7):
-                xs = [pad[base + p, r0 + i, COL0 - BORDER + kw:COL0 - BORDER + kw + 8, :] for i in range(R + 6)]
-                for kh in range(7):
-                    w = jnp.broadcast_to(dwf[k, part, kh, kw:kw + 1, :], (8, LANES))
-                    for r in range(R):
-                        term = xs[r + kh] * w
-                        accs[r] = term if accs[r] is None else accs[r] + term
-            for r in range(R):
-                ubuf[p, pl.ds((r0 + r) * 8, 8)] = accs[r] + bias
-            return 0
-
-        lax.fori_loop(0, NPL * strips, body, 0)
+        rows2 = (tile_h + 2) * tile_w
+
+        def body(j, _):
+            for strip in range(half // 12):
+                r0 = j * half + strip * 12
+                for r, acc in enumerate(taps_sum(k, 1, base + GI, r0, 12)):
+                    ubuf[GI, pl.ds(pl.multiple_of((r0 + r) * 8, 8), 8)] = acc + vec[k, 1, 0:1]
+            for strip in range(tile_h // 16):
+                for r, acc in enumerate(taps_sum(k, 0, base + 2 + j, strip * 16, 16)):
+                    ubuf[2 + j, pl.ds((strip * 16 + r) * 8, 8)] = acc + vec[k, 0, 0:1]
+
+            parts = []
+            for kw in range(0,7):
+                shifted = pad[base + j, :, COL0 - BORDER + kw:COL0 - BORDER + kw + 8, :].astype(BF16).reshape(-1, LANES)
+                for pair in range(4):
+                    parts.append(shifted[pair * 16:pair * 16 + rows2])
+            sums = jnp.dot(jnp.concatenate(parts, axis=1), diag[k, 0:3584], preferred_element_type=F32)
+            part = sums[:pix, :LANES] + sums[8:pix + 8, LANES:]
+            ubuf[j] = part + vec[k, 0, 0:1]
+            return 0
+
+        lax.fori_loop(0, 2, body, 0)
 
     LR = 64
 
@@ -352,9 +394,9 @@
 
         def body(i, _):
             v = jnp.concatenate([vbuf[i], vbuf[GI]], axis=1)
-            x = jnp.dot(v, w1[k, i], preferred_element_type=F32) + b1
+            x = jnp.dot(v, jnp.concatenate([w1[k], w1t[k, i]], axis=0), preferred_element_type=F32) + b1
             hidden = (x + x * lax.erf(x * RSQRT2X2)).astype(BF16)
-            y = lax.dot_general(hidden, w2[k, i], (((1,), (1,)), ((), ())), preferred_element_type=F32)
+            y = lax.dot_general(hidden, jnp.concatenate([pw2[k, :LANES], w2t[k, i]], axis=0), (((1,), (1,)), ((), ())), preferred_element_type=F32)
             head = (y[:, :LANES] + vec[k, 0, 3:4]) * vec[k, 0, 4:5]
             ybuf[...] += y[:, LANES:]
             new = interior(base + i)[...] + head.reshape(tile_h, tile_w, LANES)
@@ -391,6 +433,7 @@
         return body
 
     lax.fori_loop(0, groups, down_group, 0)
+    block_weights()
     lax.fori_loop(0, groups, block_group(0), 0)
     lax.fori_loop(0, groups, block_group(1), 0)
 
@@ -419,14 +462,14 @@
         return pl.pallas_call(
             functools.partial(kernel, rows_count, cols_count),
             out_shape=jax.ShapeDtypeStruct((images, tile_h, tile_w, ch), BF16),
-            in_specs=[hbm] + [vmem] * 13,
+            in_specs=[hbm] + [vmem] * 8 + [hbm, vmem, hbm, vmem, vmem],
             out_specs=hbm,
             scratch_shapes=[
                 pltpu.VMEM((images, in_w, ch_in, in_h), BF16),
-                pltpu.VMEM((in_w * LANES, LANES), BF16),
+                pltpu.VMEM((2, in_w * LANES, LANES), BF16),
                 pltpu.VMEM((in_h, LANES), BF16),
                 pltpu.VMEM((2, ch_in, LANES), F32),
-                pltpu.VMEM((2 * groups * NPL, tile_h + 2 * BORDER, ROW, LANES), F32),
+                pltpu.VMEM((2 * groups * NPL, tile_h + 2 * BORDER + 2, ROW, LANES), F32),
                 pltpu.VMEM((2, groups, 2, NPL * BORDER, tile_h, LANES), BF16),
                 pltpu.VMEM((2, groups, 2, NPL * BORDER, tile_h, LANES), BF16),
                 pltpu.VMEM((2, groups, 4, 48, LANES), BF16),
@@ -435,13 +478,20 @@
                 pltpu.VMEM((NPL, pix, LANES), F32),
                 pltpu.VMEM((NPL, pix, LANES), BF16),
                 pltpu.VMEM((pix, LANES), F32),
-                pltpu.VMEM((GI, 4 * LANES, 2 * LANES), BF16),
-                pltpu.VMEM((2, GI, 2 * LANES, hidden), BF16),
-                pltpu.VMEM((2, GI, 2 * LANES, hidden), BF16),
+                pltpu.VMEM((4 * LANES, LANES), BF16),
+                pltpu.VMEM((GI, 4 * LANES, LANES), BF16),
+                pltpu.VMEM((2, ch, hidden), BF16),
+                pltpu.VMEM((2, ch, hidden), BF16),
+                pltpu.VMEM((2, LANES, hidden), BF16),
+                pltpu.VMEM((2, GI, LANES, hidden), BF16),
+                pltpu.VMEM((2, GI, LANES, hidden), BF16),
                 pltpu.VMEM((2, 2, 7, 8, LANES), F32),
+                pltpu.VMEM((LANES, LANES), BF16),
+                pltpu.VMEM((2, 7 * 4 * LANES, 2 * LANES), BF16),
                 pltpu.VMEM((2, 2, 8, LANES), F32),
                 pltpu.VMEM((images, tile_h, tile_w, ch), BF16),
                 pltpu.SemaphoreType.DMA((images,)),
+                pltpu.SemaphoreType.DMA((2,)),
                 pltpu.SemaphoreType.DMA((groups,)),
                 pltpu.SemaphoreType.DMA((2, groups, 8)),
                 pltpu.SemaphoreType.DMA((2, groups, 8)),

time: 69.4 us -> 57.5 us (0.83)
  Pallas kernels: 65.8 us -> 54.1 us
    pallas_call x1, Pallas kernels: 65.8 us -> 54.1 us  [local_run(): pl.pallas_call(functools.partial(kernel, rows_count, cols_count), out_sha...]
where the time goes in v2:
time: 57.5 us; the launch traced here: 57.3 us
  Pallas kernels  54.1 us (94%)
  local copies, waits for them, and re-layouts  3.22 us (6%)
    pallas_call x1, Pallas kernels, local_run(): pl.pallas_call(functools.partial(kernel, rows_count, cols_count), out_sha...  54.1 us
    unnamed x1, local copies, waits for them, and re-layouts  3.22 us

profile of v2, /device:TPU:1, one launch (start us, length us, event | category | flops | bytes accessed | tf_op | source)
XLA Modules:
  0.0 57.3 jit_solution(12146685042848382920)
XLA Ops:
  0.0 54.1 %shard_map.136 = bf16[12,48,8,160]{3,2,1,0:T(8,128)(2,1)} custom-call(bf16[12,16,80,96]{3,2,1,0:T(8,128)(2,1)} %bitcast.5, bf16[1,80]{1,0:T(2,128)(2,1)} %bitcast.8, bf16[1,80]{1,0:T(2,128)(2,1)} %bitcast.9, bf16[2,2,80,160]{3,2,1,0:T(8,128)(2,1)} %down_w.1, bf16[160]{0:T(256)(128)(2,1)} %down_b.1, bf16[7,7,2,160]{3,2,1,0:T(2,128)(2,1)} %bitcast.7, ...), custom_call_target="tpu_custom_call" | custom-call | tf_op jit(solution)/shard_map/pallas_call | solution.py:462
  54.1 3.2 %copy.16 = bf16[12,48,8,160]{3,2,1,0:T(8,128)(2,1)} copy(bf16[12,48,8,160]{3,2,1,0:T(8,128)(2,1)} %shard_map.136) | data formatting | bytes 2949120

commit v3 on v2

--- a/solution.py
+++ b/solution.py
@@ -363,7 +363,7 @@
         channels = LANES + TAIL
 
         def body(t, _):
-            rows = pl.ds(pl.multiple_of(t * LR, LR), LR)
+            rows = pl.ds(t * LR, LR)
             tail = ubuf[GI, rows]
             heads = [ubuf[i, rows] for i in range(GI)]
             own = [jnp.logical_and(lane >= i * TAIL, lane < (i + 1) * TAIL) for i in range(GI)]
@@ -384,29 +384,38 @@
             vbuf[GI, rows] = (tail * pick(rs) * nwt + nbt).astype(BF16)
             return 0
 
-        lax.fori_loop(0, pix // LR, body, 0)
+        for t in range(pix // LR):
+            body(t, 0)
 
     def mlp(k, g):
         base = k * groups * NPL + g * NPL
         nxt = groups * NPL + g * NPL
         b1 = pw1_b[k:k + 1, :].astype(F32) * HALF
-        ybuf[...] = jnp.zeros(ybuf.shape, F32)
-
-        def body(i, _):
+        def up(i):
             v = jnp.concatenate([vbuf[i], vbuf[GI]], axis=1)
-            x = jnp.dot(v, jnp.concatenate([w1[k], w1t[k, i]], axis=0), preferred_element_type=F32) + b1
-            hidden = (x + x * lax.erf(x * RSQRT2X2)).astype(BF16)
+            return jnp.dot(v, jnp.concatenate([w1[k], w1t[k, i]], axis=0), preferred_element_type=F32)
+
+        def act(x):
+            x = x + b1
+            return (x + x * lax.erf(x * RSQRT2X2)).astype(BF16)
+
+        def down(i, hidden):
             y = lax.dot_general(hidden, jnp.concatenate([pw2[k, :LANES], w2t[k, i]], axis=0), (((1,), (1,)), ((), ())), preferred_element_type=F32)
             head = (y[:, :LANES] + vec[k, 0, 3:4]) * vec[k, 0, 4:5]
-            ybuf[...] += y[:, LANES:]
             new = interior(base + i)[...] + head.reshape(tile_h, tile_w, LANES)
             if k == 0:
                 interior(nxt + i)[...] = rounded(new)
             else:
                 obuf[g * GI + i, :, :, :LANES] = new.astype(BF16)
-            return 0
-
-        lax.fori_loop(0, GI, body, 0)
+            return y[:, LANES:]
+
+        x = up(0)
+        for i in range(GI):
+            hidden = act(x)
+            if i < GI - 1:
+                x = up(i + 1)
+            tail = down(i, hidden)
+            ybuf[...] = tail if i == 0 else ybuf[...] + tail
         tail = ((ybuf[...] + vec[k, 1, 3:4]) * vec[k, 1, 4:5]).reshape(tile_h, tile_w, LANES)
         new = interior(base + GI)[...] + tail
         if k == 0:

time: 57.5 us -> 48 us (0.83)
  Pallas kernels: 54.1 us -> 44.6 us
    pallas_call x1, Pallas kernels: 54.1 us -> 44.6 us  [local_run(): pl.pallas_call(functools.partial(kernel, rows_count, cols_count), out_sha...]
where the time goes in v3:
time: 48 us; the launch traced here: 47.9 us
  Pallas kernels  44.6 us (93%)
  local copies, waits for them, and re-layouts  3.22 us (7%)
    pallas_call x1, Pallas kernels, local_run(): pl.pallas_call(functools.partial(kernel, rows_count, cols_count), out_sha...  44.6 us
    unnamed x1, local copies, waits for them, and re-layouts  3.22 us

profile of v3, /device:TPU:1, one launch (start us, length us, event | category | flops | bytes accessed | tf_op | source)
XLA Modules:
  0.0 47.9 jit_solution(10354820768742671902)
XLA Ops:
  0.0 44.6 %shard_map.136 = bf16[12,48,8,160]{3,2,1,0:T(8,128)(2,1)} custom-call(bf16[12,16,80,96]{3,2,1,0:T(8,128)(2,1)} %bitcast.5, bf16[1,80]{1,0:T(2,128)(2,1)} %bitcast.8, bf16[1,80]{1,0:T(2,128)(2,1)} %bitcast.9, bf16[2,2,80,160]{3,2,1,0:T(8,128)(2,1)} %down_w.1, bf16[160]{0:T(256)(128)(2,1)} %down_b.1, bf16[7,7,2,160]{3,2,1,0:T(2,128)(2,1)} %bitcast.7, ...), custom_call_target="tpu_custom_call" | custom-call | tf_op jit(solution)/shard_map/pallas_call | solution.py:471
  44.6 3.2 %copy.16 = bf16[12,48,8,160]{3,2,1,0:T(8,128)(2,1)} copy(bf16[12,48,8,160]{3,2,1,0:T(8,128)(2,1)} %shard_map.136) | data formatting | bytes 2949120

commit v4 on v3

--- a/solution.py
+++ b/solution.py
@@ -25,9 +25,10 @@
 
 def kernel(
     rows_count, cols_count,
-    feat, norm0_w, norm0_b, down_w, down_b, dw_w, dw_b, norm_w, norm_b, pw1_w, pw1_b, pw2_w, pw2_b, layer_scale,
+    feat, norm0_w_hbm, norm0_b_hbm, down_w_hbm, down_b_hbm, dw_w_hbm, dw_b_hbm, norm_w_hbm, norm_b_hbm, pw1_w_hbm, pw1_b_hbm, pw2_w_hbm, pw2_b_hbm, scale_hbm,
     out,
-    fv, ab, sel, norm0, pad, hsend, hrecv, csend, crecv, cstage, ubuf, vbuf, ybuf, wd, wdt, pw1, pw2, w1, w1t, w2t, dwf, eye, diag, vec, obuf,
+    norm0_w, norm0_b, down_w, down_b, dw_w, dw_b, norm_w, norm_b, pw1, pw1_b, pw2, pw2_b, layer_scale,
+    fv, ab, sel, norm0, pad, hsend, hrecv, csend, crecv, cstage, ubuf, vbuf, ybuf, wd, wdt, w1, w1t, w2t, dwf, eye, diag, vec, obuf,
     feat_sem, weight_sem, out_sem, send_sem, recv_sem,
 ):
     images, in_w, ch_in, in_h = fv.shape
@@ -59,8 +60,10 @@
         return {"sh": my_row + dr, "sw": my_col + dc}
 
     feat_copies = [pltpu.make_async_copy(feat.at[i], fv.at[i], feat_sem.at[i]) for i in range(images)]
-    weight_copies = [pltpu.make_async_copy(pw1_w, pw1, weight_sem.at[0]), pltpu.make_async_copy(pw2_w, pw2, weight_sem.at[1])]
-    for copy in feat_copies[:GI] + weight_copies + feat_copies[GI:]:
+    weights_hbm = [norm0_w_hbm, norm0_b_hbm, down_w_hbm, down_b_hbm, dw_w_hbm, dw_b_hbm, norm_w_hbm, norm_b_hbm, pw1_w_hbm, pw1_b_hbm, pw2_w_hbm, pw2_b_hbm, scale_hbm]
+    weights_here = [norm0_w, norm0_b, down_w, down_b, dw_w, dw_b, norm_w, norm_b, pw1, pw1_b, pw2, pw2_b, layer_scale]
+    weight_copies = [pltpu.make_async_copy(far, near, weight_sem.at[n]) for n, (far, near) in enumerate(zip(weights_hbm, weights_here))]
+    for copy in weight_copies[:4] + feat_copies[:GI] + weight_copies[4:] + feat_copies[GI:]:
         copy.start()
 
     barrier = pltpu.get_barrier_semaphore()
@@ -91,6 +94,8 @@
     col_id = lax.broadcasted_iota(jnp.int32, sel.shape, 1)
     picked = jnp.where(row_id < tile_h, 2 * row_id, 2 * (row_id - tile_h) + 1)
     sel[...] = jnp.where(col_id == picked, 1.0, 0.0).astype(BF16)
+    for copy in weight_copies[:4]:
+        copy.wait()
     norm0[0] = jnp.broadcast_to(norm0_w[...].astype(F32), (LANES, ch_in)).T
     norm0[1] = jnp.broadcast_to(norm0_b[...].astype(F32), (LANES, ch_in)).T
     cstage[...] = jnp.zeros(cstage.shape, F32)
@@ -114,8 +119,21 @@
             wdt[slot, pl.ds(tap * LANES + ch_in, LANES - ch_in)] = zeros
 
     def block_weights():
-        for copy in weight_copies:
+        for copy in weight_copies[4:]:
             copy.wait()
+        for kh in range(7):
+            for kw in range(7):
+                taps = dw_w[kh, kw].astype(F32)
+                tails = jnp.concatenate([taps[:, LANES:]] * GI, axis=1)
+                for k in range(2):
+                    dwf[k, 0, kh, kw:kw + 1] = taps[k:k + 1, :LANES]
+                    dwf[k, 1, kh, kw:kw + 1] = tails[k:k + 1]
+        names = [dw_b, norm_w, norm_b, pw2_b, layer_scale]
+        for k in range(2):
+            for j, ref in enumerate(names):
+                head, tail = split(ref[k:k + 1, :])
+                vec[k, 0, j:j + 1] = head
+                vec[k, 1, j:j + 1] = tail
         for k in range(2):
             w1[k] = (pw1[k, :LANES].astype(F32) * HALF).astype(BF16)
             up_tail = (pw1[k, LANES:].astype(F32) * HALF).astype(BF16)
@@ -125,14 +143,6 @@
                     w1t[k, slot, rows] = up_tail if other == slot else jnp.zeros(up_tail.shape, BF16)
                     w2t[k, slot, rows] = pw2[k, LANES:] if other == slot else jnp.zeros(up_tail.shape, BF16)
         lax.fori_loop(0, 7, spread, 0)
-
-    for kh in range(7):
-        for kw in range(7):
-            taps = dw_w[kh, kw].astype(F32)
-            tails = jnp.concatenate([taps[:, LANES:]] * GI, axis=1)
-            for k in range(2):
-                dwf[k, 0, kh, kw:kw + 1] = taps[k:k + 1, :LANES]
-                dwf[k, 1, kh, kw:kw + 1] = tails[k:k + 1]
 
     eye[...] = jnp.where(lax.broadcasted_iota(jnp.int32, eye.shape, 0) == lax.broadcasted_iota(jnp.int32, eye.shape, 1), 1.0, 0.0).astype(BF16)
 
@@ -154,12 +164,6 @@
         row = row.astype(F32)
         return row[:, :LANES], jnp.concatenate([row[:, LANES:]] * GI, axis=1)
 
-    names = [dw_b, norm_w, norm_b, pw2_b, layer_scale]
-    for k in range(2):
-        for j, ref in enumerate(names):
-            head, tail = split(ref[k:k + 1, :])
-            vec[k, 0, j:j + 1] = head
-            vec[k, 1, j:j + 1] = tail
     head, tail = split(down_b[...].reshape(1, -1))
     vec[0, 0, 5:6] = head
     vec[0, 1, 5:6] = tail
@@ -197,12 +201,9 @@
         for q in (2, 3):
             first = 0 if q == 2 else tile_w - BORDER
 
-            def fill(p, _):
+            for p in range(NPL):
                 for j in range(BORDER):
                     hsend[k, g, q - 2, p * BORDER + j] = column(base + p, 0, first + j, tile_h)[...].astype(BF16)
-                return 0
-
-            lax.fori_loop(0, NPL, fill, 0)
         for q in range(4, 8):
             dr, dc = steps[q]
             first = 0 if dc < 0 else tile_w - BORDER
@@ -223,12 +224,9 @@
 
             @pl.when(exists(q))
             def _():
-                def put(p, _):
+                for p in range(NPL):
                     for j in range(BORDER):
                         column(base + p, 0, first + j, tile_h)[...] = hrecv[k, g, q - 2, p * BORDER + j].astype(F32)
-                    return 0
-
-                lax.fori_loop(0, NPL, put, 0)
         for q in range(4, 8):
             dr, dc = steps[q]
             first = -BORDER if dc < 0 else tile_w
@@ -466,14 +464,17 @@
         ch, hidden = pw1_w.shape[1:]
         groups = images // GI
         pix = tile_h * tile_w
-        vmem = pl.BlockSpec(memory_space=pltpu.VMEM)
+        weights = [
+            norm0_w.reshape(1, -1), norm0_b.reshape(1, -1), down_w, down_b, dw_w.transpose(1, 2, 0, 3), dw_b,
+            norm_w, norm_b, pw1_w, pw1_b, pw2_w.transpose(0, 2, 1), pw2_b, layer_scale,
+        ]
         hbm = pl.BlockSpec(memory_space=pl.ANY)
         return pl.pallas_call(
             functools.partial(kernel, rows_count, cols_count),
             out_shape=jax.ShapeDtypeStruct((images, tile_h, tile_w, ch), BF16),
-            in_specs=[hbm] + [vmem] * 8 + [hbm, vmem, hbm, vmem, vmem],
+            in_specs=[hbm] * (1 + len(weights)),
             out_specs=hbm,
-            scratch_shapes=[
+            scratch_shapes=[pltpu.VMEM(w.shape, BF16) for w in weights] + [
                 pltpu.VMEM((images, in_w, ch_in, in_h), BF16),
                 pltpu.VMEM((2, in_w * LANES, LANES), BF16),
                 pltpu.VMEM((in_h, LANES), BF16),
@@ -489,8 +490,6 @@
                 pltpu.VMEM((pix, LANES), F32),
                 pltpu.VMEM((4 * LANES, LANES), BF16),
                 pltpu.VMEM((GI, 4 * LANES, LANES), BF16),
-                pltpu.VMEM((2, ch, hidden), BF16),
-                pltpu.VMEM((2, ch, hidden), BF16),
                 pltpu.VMEM((2, LANES, hidden), BF16),
                 pltpu.VMEM((2, GI, LANES, hidden), BF16),
                 pltpu.VMEM((2, GI, LANES, hidden), BF16),
@@ -500,15 +499,12 @@
                 pltpu.VMEM((2, 2, 8, LANES), F32),
                 pltpu.VMEM((images, tile_h, tile_w, ch), BF16),
                 pltpu.SemaphoreType.DMA((images,)),
-                pltpu.SemaphoreType.DMA((2,)),
+                pltpu.SemaphoreType.DMA((len(weights),)),
                 pltpu.SemaphoreType.DMA((groups,)),
                 pltpu.SemaphoreType.DMA((2, groups, 8)),
                 pltpu.SemaphoreType.DMA((2, groups, 8)),
             ],
             compiler_params=pltpu.CompilerParams(collective_id=0, has_side_effects=True, vmem_limit_bytes=63 * 1024 * 1024),
-        )(
-            feat_map.transpose(0, 2, 3, 1), norm0_w.reshape(1, -1), norm0_b.reshape(1, -1), down_w, down_b, dw_w.transpose(1, 2, 0, 3), dw_b,
-            norm_w, norm_b, pw1_w, pw1_b, pw2_w.transpose(0, 2, 1), pw2_b, layer_scale,
-        )
+        )(feat_map.transpose(0, 2, 3, 1), *weights)
 
     return jax.shard_map(local_run, mesh=mesh, in_specs=(act_spec,) + (P(),) * 13, out_specs=act_spec, check_vma=False)

time: 48 us -> 46.4 us (0.967)
  Pallas kernels: 44.6 us -> 43 us
    pallas_call x1, Pallas kernels: 44.6 us -> 43 us  [local_run(): pl.pallas_call(functools.partial(kernel, rows_count, cols_count), out_sha...]
where the time goes in v4:
time: 46.4 us; the launch traced here: 46.2 us
  Pallas kernels  43 us (93%)
  local copies, waits for them, and re-layouts  3.22 us (7%)
    pallas_call x1, Pallas kernels, local_run(): pl.pallas_call(functools.partial(kernel, rows_count, cols_count), out_sha...  43 us
    unnamed x1, local copies, waits for them, and re-layouts  3.22 us

profile of v4, /device:TPU:1, one launch (start us, length us, event | category | flops | bytes accessed | tf_op | source)
XLA Modules:
  0.0 46.2 jit_solution(17596230717603393236)
XLA Ops:
  0.0 43.0 %shard_map.136 = bf16[12,48,8,160]{3,2,1,0:T(8,128)(2,1)} custom-call(bf16[12,16,80,96]{3,2,1,0:T(8,128)(2,1)} %bitcast.5, bf16[1,80]{1,0:T(2,128)(2,1)} %bitcast.8, bf16[1,80]{1,0:T(2,128)(2,1)} %bitcast.9, bf16[2,2,80,160]{3,2,1,0:T(8,128)(2,1)} %down_w_hbm.1, bf16[160]{0:T(256)(128)(2,1)} %down_b_hbm.1, bf16[7,7,2,160]{3,2,1,0:T(2,128)(2,1)} %bitcast.7, ...), custom_call_target="tpu_custom_call" | custom-call | tf_op jit(solution)/shard_map/pallas_call | solution.py:472
  43.0 3.2 %copy.16 = bf16[12,48,8,160]{3,2,1,0:T(8,128)(2,1)} copy(bf16[12,48,8,160]{3,2,1,0:T(8,128)(2,1)} %shard_map.136) | data formatting | bytes 2949120

commit v5 on v4

--- a/solution.py
+++ b/solution.py
@@ -40,6 +40,7 @@
     has_left, has_right = my_col > 0, my_col < cols_count - 1
 
     steps = [(-1, 0), (1, 0), (0, -1), (0, 1), (-1, -1), (-1, 1), (1, -1), (1, 1)]
+    steps += [(0, -1), (0, 1)]
     row_ok = {-1: has_up, 0: None, 1: has_down}
     col_ok = {-1: has_left, 0: None, 1: has_right}
 
@@ -53,7 +54,7 @@
 
     def opposite(q):
         dr, dc = steps[q]
-        return steps.index((-dr, -dc))
+        return q ^ 1 if dr == 0 else steps.index((-dr, -dc))
 
     def device(q):
         dr, dc = steps[q]
@@ -109,14 +110,17 @@
             parts = parts + [jnp.zeros((rows, TAIL * (GI - 1 - slot)), tail.dtype)]
         return jnp.concatenate(parts, axis=1)
 
-    for tap in range(4):
-        taps = down_w[tap // 2, tap % 2].astype(F32)
-        zeros = jnp.zeros((LANES - ch_in, LANES), BF16)
-        wd[pl.ds(tap * LANES, ch_in)] = taps[:, :LANES].astype(BF16)
-        wd[pl.ds(tap * LANES + ch_in, LANES - ch_in)] = zeros
+    for kh in range(2):
+        zeros = jnp.zeros((2 * LANES - 2 * ch_in, LANES), BF16)
+        wd[pl.ds(kh * 2 * LANES + 2 * ch_in, 2 * LANES - 2 * ch_in)] = zeros
+        for kw in range(2):
+            taps = down_w[kh, kw].astype(F32)
+            rows = pl.ds(kh * 2 * LANES + kw * ch_in, ch_in)
+            wd[rows] = taps[:, :LANES].astype(BF16)
+            for slot in range(GI):
+                wdt[slot, rows] = tail_at(taps[:, LANES:], slot).astype(BF16)
         for slot in range(GI):
-            wdt[slot, pl.ds(tap * LANES, ch_in)] = tail_at(taps[:, LANES:], slot).astype(BF16)
-            wdt[slot, pl.ds(tap * LANES + ch_in, LANES - ch_in)] = zeros
+            wdt[slot, pl.ds(kh * 2 * LANES + 2 * ch_in, 2 * LANES - 2 * ch_in)] = zeros
 
     def block_weights():
         for copy in weight_copies[4:]:
@@ -173,6 +177,9 @@
     def column(plane, row, col, count):
         return flat.at[plane, pl.ds((BORDER + row) * ROW + COL0 + col, count, stride=ROW), :]
 
+    def side_rows(q):
+        return pl.ds(0, 2 * BORDER) if q >= 8 else pl.ds(2 * BORDER, (NPL - 2) * BORDER)
+
     def messages(k, g):
         base = k * groups * NPL + g * NPL
         planes = pl.ds(base, NPL)
@@ -185,8 +192,8 @@
                 src = pad.at[planes, pl.ds(first, BORDER), pl.ds(COL0, tile_w), :]
                 dst = pad.at[planes, pl.ds(land, BORDER), pl.ds(COL0, tile_w), :]
             elif dr == 0:
-                src = hsend.at[k, g, q - 2]
-                dst = hrecv.at[k, g, there - 2]
+                src = hsend.at[k, g, q % 2, side_rows(q)]
+                dst = hrecv.at[k, g, there % 2, side_rows(q)]
             else:
                 src = csend.at[k, g, q - 4]
                 dst = crecv.at[k, g, there - 4]
@@ -195,15 +202,23 @@
                 device_id=device(q), device_id_type=MESH))
         return copies
 
-    def send(k, g):
-        base = k * groups * NPL + g * NPL
+    def fill_sides(k, g, planes):
+        base = k * groups * NPL + g * NPL
+        for side, first in ((0, 0), (1, tile_w - BORDER)):
+            for p in planes:
+                for j in range(BORDER):
+                    hsend[k, g, side, p * BORDER + j] = column(base + p, 0, first + j, tile_h)[...].astype(BF16)
+
+    def send_early(k, g):
         copies = messages(k, g)
-        for q in (2, 3):
-            first = 0 if q == 2 else tile_w - BORDER
-
-            for p in range(NPL):
-                for j in range(BORDER):
-                    hsend[k, g, q - 2, p * BORDER + j] = column(base + p, 0, first + j, tile_h)[...].astype(BF16)
+        fill_sides(k, g, range(2))
+        for q in (8, 9):
+            pl.when(exists(q))(copies[q].start)
+
+    def send_late(k, g):
+        base = k * groups * NPL + g * NPL
+        copies = messages(k, g)
+        fill_sides(k, g, range(2, NPL))
         for q in range(4, 8):
             dr, dc = steps[q]
             first = 0 if dc < 0 else tile_w - BORDER
@@ -212,12 +227,12 @@
                 for j in range(BORDER):
                     cstage[pl.ds((p * BORDER + j) * BORDER, BORDER)] = column(base + p, row, first + j, BORDER)[...]
             csend[k, g, q - 4] = cstage[...].astype(BF16)
-        for q in range(8):
+        for q in (2, 3, 4, 5, 6, 7, 0, 1):
             pl.when(exists(q))(copies[q].start)
 
     def receive(k, g):
         base = k * groups * NPL + g * NPL
-        for q in range(8):
+        for q in range(len(steps)):
             pl.when(exists(q))(_wait_recv(k, g, q))
         for q in (2, 3):
             first = -BORDER if q == 2 else tile_w
@@ -246,7 +261,7 @@
             land = 0 if dr < 0 else BORDER + tile_h
             dst = pad.at[pl.ds(base, NPL), pl.ds(land, BORDER), pl.ds(COL0, tile_w), :]
         elif dr == 0:
-            dst = hrecv.at[k, g, q - 2]
+            dst = hrecv.at[k, g, q % 2, side_rows(q)]
         else:
             dst = crecv.at[k, g, q - 4]
 
@@ -259,7 +274,7 @@
 
     def wait_send(k, g):
         copies = messages(k, g)
-        for q in range(8):
+        for q in range(len(steps)):
             pl.when(exists(q))(copies[q].wait_send)
 
     def interior(plane):
@@ -277,11 +292,17 @@
             centered = x - mean
             var = jnp.sum(centered * centered, axis=0, keepdims=True) * (1.0 / ch_in)
             a = centered * lax.rsqrt(var + LN_EPS) * norm0[0, :, :in_h] + norm0[1, :, :in_h]
-            ab[slot, pl.ds(w * LANES, ch_in), :in_h] = a.astype(BF16)
+            ab[slot, pl.ds(w * ch_in, ch_in), :in_h] = a.astype(BF16)
 
     def down_conv(g, i, slot):
         turned = lax.dot_general(sel[...], ab[slot], (((1,), (1,)), ((), ())), preferred_element_type=F32).astype(BF16)
-        taps = [jnp.concatenate([turned[:tile_h, w * 2 * LANES:(w + 1) * 2 * LANES], turned[tile_h:, w * 2 * LANES:(w + 1) * 2 * LANES]], axis=1) for w in range(tile_w)]
+        pair = 2 * ch_in
+        taps = []
+        for w in range(tile_w):
+            window = turned[:, w * pair:min(w * pair + 2 * LANES, turned.shape[1])]
+            if window.shape[1] < 2 * LANES:
+                window = jnp.concatenate([window, jnp.zeros((in_h, 2 * LANES - window.shape[1]), BF16)], axis=1)
+            taps.append(jnp.concatenate([window[:tile_h], window[tile_h:]], axis=1))
         weights = jnp.concatenate([wd[...], wdt[i]], axis=1)
         d = jnp.dot(jnp.concatenate(taps, axis=0), weights, preferred_element_type=F32)
         head = rounded(d[:, :LANES] + vec[0, 0, 5:6])
@@ -292,17 +313,13 @@
     def down_group(g, _):
         ybuf[...] = jnp.zeros(ybuf.shape, F32)
 
-        def two(j, _):
+        def two(j):
             down_norm(g, 2 * j, 0)
             down_norm(g, 2 * j + 1, 1)
             down_conv(g, 2 * j, 0)
             down_conv(g, 2 * j + 1, 1)
-            return 0
-
-        lax.fori_loop(0, GI // 2, two, 0)
-        tail = rounded(ybuf[...] + vec[0, 1, 5:6])
-        for w in range(tile_w):
-            column(g * NPL + GI, 0, w, tile_h)[...] = tail[w * tile_h:(w + 1) * tile_h]
+
+        two(0)
 
         @pl.when(g == 0)
         def _():
@@ -311,7 +328,12 @@
                 count = count + exists(q).astype(jnp.int32)
             pl.semaphore_wait(barrier, count)
 
-        send(0, g)
+        send_early(0, g)
+        two(1)
+        tail = rounded(ybuf[...] + vec[0, 1, 5:6])
+        for w in range(tile_w):
+            column(g * NPL + GI, 0, w, tile_h)[...] = tail[w * tile_h:(w + 1) * tile_h]
+        send_late(0, g)
         return 0
 
     half = tile_h // 2
@@ -433,7 +455,8 @@
             norm(k)
             mlp(k, g)
             if k == 0:
-                send(1, g)
+                send_early(1, g)
+                send_late(1, g)
             else:
                 out_copy(g).start()
             return 0
@@ -476,7 +499,7 @@
             out_specs=hbm,
             scratch_shapes=[pltpu.VMEM(w.shape, BF16) for w in weights] + [
                 pltpu.VMEM((images, in_w, ch_in, in_h), BF16),
-                pltpu.VMEM((2, in_w * LANES, LANES), BF16),
+                pltpu.VMEM((2, in_w * ch_in, LANES), BF16),
                 pltpu.VMEM((in_h, LANES), BF16),
                 pltpu.VMEM((2, ch_in, LANES), F32),
                 pltpu.VMEM((2 * groups * NPL, tile_h + 2 * BORDER + 2, ROW, LANES), F32),
@@ -501,8 +524,8 @@
                 pltpu.SemaphoreType.DMA((images,)),
                 pltpu.SemaphoreType.DMA((len(weights),)),
                 pltpu.SemaphoreType.DMA((groups,)),
-                pltpu.SemaphoreType.DMA((2, groups, 8)),
-                pltpu.SemaphoreType.DMA((2, groups, 8)),
+                pltpu.SemaphoreType.DMA((2, groups, 10)),
+                pltpu.SemaphoreType.DMA((2, groups, 10)),
             ],
             compiler_params=pltpu.CompilerParams(collective_id=0, has_side_effects=True, vmem_limit_bytes=63 * 1024 * 1024),
         )(feat_map.transpose(0, 2, 3, 1), *weights)

time: 46.4 us -> 45.1 us (0.972)
  Pallas kernels: 43 us -> 41.7 us
    pallas_call x1, Pallas kernels: 43 us -> 41.7 us  [local_run(): pl.pallas_call(functools.partial(kernel, rows_count, cols_count), out_sha...]
where the time goes in v5:
time: 45.1 us; the launch traced here: 44.9 us
  Pallas kernels  41.7 us (92%)
  local copies, waits for them, and re-layouts  3.22 us (7%)
    pallas_call x1, Pallas kernels, local_run(): pl.pallas_call(functools.partial(kernel, rows_count, cols_count), out_sha...  41.7 us
    unnamed x1, local copies, waits for them, and re-layouts  3.22 us

profile of v5, /device:TPU:1, one launch (start us, length us, event | category | flops | bytes accessed | tf_op | source)
XLA Modules:
  0.0 44.9 jit_solution(10055578169744483967)
XLA Ops:
  0.0 41.7 %shard_map.136 = bf16[12,48,8,160]{3,2,1,0:T(8,128)(2,1)} custom-call(bf16[12,16,80,96]{3,2,1,0:T(8,128)(2,1)} %bitcast.5, bf16[1,80]{1,0:T(2,128)(2,1)} %bitcast.8, bf16[1,80]{1,0:T(2,128)(2,1)} %bitcast.9, bf16[2,2,80,160]{3,2,1,0:T(8,128)(2,1)} %down_w_hbm.1, bf16[160]{0:T(256)(128)(2,1)} %down_b_hbm.1, bf16[7,7,2,160]{3,2,1,0:T(2,128)(2,1)} %bitcast.7, ...), custom_call_target="tpu_custom_call" | custom-call | tf_op jit(solution)/shard_map/pallas_call | solution.py:495
  41.7 3.2 %copy.16 = bf16[12,48,8,160]{3,2,1,0:T(8,128)(2,1)} copy(bf16[12,48,8,160]{3,2,1,0:T(8,128)(2,1)} %shard_map.136) | data formatting | bytes 2949120

commit v6 on v5

--- a/solution.py
+++ b/solution.py
@@ -64,7 +64,7 @@
     weights_hbm = [norm0_w_hbm, norm0_b_hbm, down_w_hbm, down_b_hbm, dw_w_hbm, dw_b_hbm, norm_w_hbm, norm_b_hbm, pw1_w_hbm, pw1_b_hbm, pw2_w_hbm, pw2_b_hbm, scale_hbm]
     weights_here = [norm0_w, norm0_b, down_w, down_b, dw_w, dw_b, norm_w, norm_b, pw1, pw1_b, pw2, pw2_b, layer_scale]
     weight_copies = [pltpu.make_async_copy(far, near, weight_sem.at[n]) for n, (far, near) in enumerate(zip(weights_hbm, weights_here))]
-    for copy in weight_copies[:4] + feat_copies[:GI] + weight_copies[4:] + feat_copies[GI:]:
+    for copy in weight_copies[:4] + feat_copies[:GI]:
         copy.start()
 
     barrier = pltpu.get_barrier_semaphore()
@@ -146,7 +146,8 @@
                     rows = pl.ds(TAIL * other, TAIL)
                     w1t[k, slot, rows] = up_tail if other == slot else jnp.zeros(up_tail.shape, BF16)
                     w2t[k, slot, rows] = pw2[k, LANES:] if other == slot else jnp.zeros(up_tail.shape, BF16)
-        lax.fori_loop(0, 7, spread, 0)
+        for kw in range(7):
+            spread(kw, 0)
 
     eye[...] = jnp.where(lax.broadcasted_iota(jnp.int32, eye.shape, 0) == lax.broadcasted_iota(jnp.int32, eye.shape, 1), 1.0, 0.0).astype(BF16)
 
@@ -155,11 +156,11 @@
         for k in range(2):
             for kh in range(8):
                 if kh < 7:
-                    tap = jnp.broadcast_to(dwf[k, 0, kh, pl.ds(kw, 1)], (16, LANES)).astype(BF16)
+                    tap = jnp.broadcast_to(dwf[k, 0, kh, kw:kw + 1], (16, LANES)).astype(BF16)
                     block = unit * jnp.concatenate([tap] * (LANES // 16), axis=0)
                 else:
                     block = jnp.zeros((LANES, LANES), BF16)
-                diag[k, pl.ds(pl.multiple_of(kw * 4 * LANES, LANES) + kh // 2 * LANES, LANES), kh % 2 * LANES:(kh % 2 + 1) * LANES] = block
+                diag[k, pl.ds((kw * 4 + kh // 2) * LANES, LANES), kh % 2 * LANES:(kh % 2 + 1) * LANES] = block
         return 0
 
     pad[:, tile_h + 2 * BORDER:] = jnp.zeros((pad.shape[0], 2, ROW, LANES), F32)
@@ -311,6 +312,17 @@
         ybuf[...] += d[:, LANES:]
 
     def down_group(g, _):
+        @pl.when(g == 0)
+        def _():
+            for copy in weight_copies[4:]:
+                copy.start()
+
+        @pl.when(g < groups - 1)
+        def _():
+            for i in range(GI):
+                img = (g + 1) * GI + i
+                pltpu.make_async_copy(feat.at[img], fv.at[img], feat_sem.at[img]).start()
+
         ybuf[...] = jnp.zeros(ybuf.shape, F32)
 
         def two(j):

time: 45.1 us -> 44.9 us (level)
  no operation moved by 1% of the time
where the time goes in v6:
time: 44.9 us; the launch traced here: 44.7 us
  Pallas kernels  41.5 us (92%)
  local copies, waits for them, and re-layouts  3.22 us (7%)
    pallas_call x1, Pallas kernels, local_run(): pl.pallas_call(functools.partial(kernel, rows_count, cols_count), out_sha...  41.5 us
    unnamed x1, local copies, waits for them, and re-layouts  3.22 us

profile of v6, /device:TPU:1, one launch (start us, length us, event | category | flops | bytes accessed | tf_op | source)
XLA Modules:
  0.0 44.7 jit_solution(11011971450597162166)
XLA Ops:
  0.0 41.5 %shard_map.136 = bf16[12,48,8,160]{3,2,1,0:T(8,128)(2,1)} custom-call(bf16[12,16,80,96]{3,2,1,0:T(8,128)(2,1)} %bitcast.5, bf16[1,80]{1,0:T(2,128)(2,1)} %bitcast.8, bf16[1,80]{1,0:T(2,128)(2,1)} %bitcast.9, bf16[2,2,80,160]{3,2,1,0:T(8,128)(2,1)} %down_w_hbm.1, bf16[160]{0:T(256)(128)(2,1)} %down_b_hbm.1, bf16[7,7,2,160]{3,2,1,0:T(2,128)(2,1)} %bitcast.7, ...), custom_call_target="tpu_custom_call" | custom-call | tf_op jit(solution)/shard_map/pallas_call | solution.py:507
  41.5 3.2 %copy.16 = bf16[12,48,8,160]{3,2,1,0:T(8,128)(2,1)} copy(bf16[12,48,8,160]{3,2,1,0:T(8,128)(2,1)} %shard_map.136) | data formatting | bytes 2949120
